TPU v7x, 32 devices: a whole 2x2x4 slice. The times are simulated.
32 devices in a mesh: freq: 8 (over z, core), cell: 4 (over y, x).
Axes of the slice: x: 2, y: 2, z: 4, core: 2. Of those that a mesh axis runs over, the one named last changes fastest.
Arguments:
- covariance: bfloat16 [256, 2, 256, 256], P('freq', None, 'cell'), may hold values from -4 to 6, as said below
- replica: bfloat16 [256, 2, 256, 2048], P('freq', None, None, 'cell'), may hold values from -0.25 to 0.25
- transmission: bfloat16 [256, 2048], P('freq', 'cell'), may hold values from 0.29882812 to 3
Outputs:
- ambiguity: float32 [2048], P('cell')
- relative: float32 [2048], P('cell')
Inputs may be any that keep to these rules, and one draw needn't show every extreme that they name: Each covariance[f, 0] + i covariance[f, 1] is exactly Hermitian, also after rounding to bfloat16; before rounding all its eigenvalues are at least 0.5.
All inputs are finite; a program needn't handle non-finite values.
Results may differ from a plain program's by a relative error of at most 0.0003.
Values may be sent and summed in bfloat16 or wider, within the bound.
A program may use at most 384 MiB of HBM per device.

v0:
```python
import jax
import jax.numpy as jnp
from jax import lax
from jax.sharding import PartitionSpec as P


def quadratic(cov_piece, col_fields, row_fields):
    count, _, rows, depths = cov_piece.shape
    stacked = cov_piece.reshape(count, 2 * rows, depths)
    first = jnp.einsum(
        "fij,fjc->fic", stacked, col_fields[:, 0], preferred_element_type=jnp.float32
    )
    second = jnp.einsum(
        "fij,fjc->fic", stacked, col_fields[:, 1], preferred_element_type=jnp.float32
    )
    image_re = first[:, :rows] - second[:, rows:]
    image_im = first[:, rows:] + second[:, :rows]
    return jnp.sum(row_fields[:, 0] * image_re + row_fields[:, 1] * image_im, axis=1)


def shards(covariance, replica, transmission):
    freq_total = covariance.shape[0] * lax.axis_size("freq")
    power = quadratic(lax.all_gather(covariance, "cell", axis=2, tiled=True), replica, replica)
    amplitude = transmission.astype(jnp.float32)
    partial_value = jnp.sum(amplitude * amplitude * power, axis=0)
    partial_value = partial_value / jnp.float32(freq_total)
    ambiguity = lax.psum(partial_value, "freq")
    peak = lax.pmax(jnp.max(ambiguity), "cell")
    relative = ambiguity / jnp.maximum(peak, jnp.float32(1.0))
    return (ambiguity, relative)


def solution(mesh):
    return jax.shard_map(
        shards,
        mesh=mesh,
        in_specs=(P("freq", None, "cell", None), P("freq", None, None, "cell"), P("freq", "cell")),
        out_specs=(P("cell"), P("cell")),
        check_vma=False,
    )
```

profile of v0, /device:TPU:0, one launch (start us, length us, event | category | flops | bytes accessed | tf_op | source)
XLA Modules:
  0.0 197.6 jit_solution(6672672013921874193)
XLA Ops:
  7.2 0.0 all-gather.2.cloned.1.call-start
  7.2 0.7 all-gather.2.cloned.1.call-update
  7.9 92.2 %all-gather.2.cloned.1.call-done = bf16[32,2,256,256]{3,2,1,0:T(8,128)(2,1)} async-done(((bf16[32,2,64,256]{3,2,1,0:T(8,128)(2,1)}), bf16[32,2,256,256]{3,2,1,0:T(8,128)(2,1)}) %all-gather.2.cloned.1.call-update) | async-done | bytes 8388624 | tf_op jit(solution)/shard_map/all_gather | solution.py:23
  100.1 17.7 %fusion.4 = f32[32,512,512]{2,1,0:T(8,128)} fusion(bf16[32,512,256]{2,1,0:T(8,128)(2,1)} %bitcast.15, bf16[32,2,256,512]{3,2,1,0:T(8,128)(2,1)} %param.4), kind=kOutput, calls=%fused_computation.6 | convolution fusion | flops 4294967296 | bytes 50331648 | tf_op jit(solution)/shard_map/fij,fjc->fic/dot_general | solution.py:13
  117.8 17.7 %fusion.6 = f32[32,512,512]{2,1,0:T(8,128)} fusion(bf16[32,512,256]{2,1,0:T(8,128)(2,1)} %bitcast.16, bf16[32,2,256,512]{3,2,1,0:T(8,128)(2,1)} %param.4), kind=kOutput, calls=%fused_computation.8 | convolution fusion | flops 4294967296 | bytes 50331648 | tf_op jit(solution)/shard_map/fij,fjc->fic/dot_general | solution.py:10
  135.5 0.0 copy-start
  135.5 27.6 %fusion.2 = f32[32,512]{1,0:T(8,128)S(1)} fusion(f32[32,512,512]{2,1,0:T(8,128)} %fusion.4, f32[32,512,512]{2,1,0:T(8,128)} %fusion.6, bf16[32,2,256,512]{3,2,1,0:T(8,128)(2,1)} %param.4), kind=kLoop, calls=%fused_computation.3 | loop fusion | flops 33538048 | bytes 83951616 | tf_op jit(solution)/shard_map/reduce_sum | solution.py:18
  163.1 0.0 copy-done
  163.2 16.2 %psum.7 = f32[512]{0:T(512)S(1)} all-reduce(f32[512]{0:T(512)S(1)} %broadcast_multiply_fusion), channel_id=1, replica_groups=mesh['freq'=8,'cell'=4] {'freq'}, use_global_device_ids=true, to_apply=%region_2.0 | all-reduce | flops 512 | bytes 4096 | tf_op jit(solution)/shard_map/psum | solution.py:27
  179.4 0.0 copy-start.1
  179.4 0.6 reduce_max.9
  180.0 9.5 %pmax.7 = f32[]{:T(128)} all-reduce(f32[]{:T(128)} %reduce_max.9), channel_id=1, replica_groups=mesh['freq'=8,'cell'=4] {'cell'}, use_global_device_ids=true, to_apply=%region_4.0 | all-reduce | flops 1 | bytes 8 | tf_op jit(solution)/shard_map/pmax | solution.py:28
  190.2 0.6 broadcast_divide_fusion
  190.8 0.0 copy-done.1
  (2 shorter events, 0.0 us)
Async XLA Ops:
  7.2 92.9 %all-gather.2.cloned.1.call-start = ((), (), s32[]{:S(2)}) async-start(), calls=%async_computation | async-start | bytes 10485760 | tf_op jit(solution)/shard_map/all_gather | solution.py:23
  135.5 27.6 %copy-start = (bf16[32,512]{1,0:T(8,128)(2,1)S(1)}, bf16[32,512]{1,0:T(8,128)(2,1)}, u32[]{:S(2)}) copy-start(bf16[32,512]{1,0:T(8,128)(2,1)} %param.5) | copy-start | bytes 98308
  179.4 11.4 %copy-start.1 = (f32[512]{0:T(512)}, f32[512]{0:T(512)S(1)}, u32[]{:S(2)}) copy-start(f32[512]{0:T(512)S(1)} %psum.7) | copy-start | bytes 6148
Sparse Core Ops, SparseCore 0:
  9.8 90.1 all-gather.1
where the time goes:
time: 198 us
  waiting for transfers between devices  92.8 us (47%)
  matrix products  35.5 us (18%)
  other arithmetic  28.8 us (15%)
  blocking collectives  25.7 us (13%)
  between operations  14.7 us (7%)
    all_gather x1, waiting for transfers between devices, shards(): lax.all_gather(covariance, 'cell', axis=2, tiled=True)  92.2 us
    reduce_sum x1, other arithmetic, quadratic(): jnp.sum(row_fields[:, 0] * image_re + row_fields[:, 1] * image_im, axis=1)  27.6 us
    dot_general x1, matrix products, quadratic(): jnp.einsum('fij,fjc->fic', stacked, col_fields[:, 1], preferred_element_t...  17.7 us
    dot_general x1, matrix products, quadratic(): jnp.einsum('fij,fjc->fic', stacked, col_fields[:, 0], preferred_element_t...  17.7 us
    psum x1, blocking collectives, shards(): ambiguity = lax.psum(partial_value, 'freq')  16.2 us
    pmax x1, blocking collectives, shards(): peak = lax.pmax(jnp.max(ambiguity), 'cell')  9.54 us
  transfers between devices with their start and end apart: 1, of which 1 were waited for; matrix products, arithmetic and copies ran while one was open for 0% of the time, Pallas kernels for 0%

commit v1 on v0

--- a/solution.py
+++ b/solution.py
@@ -24,7 +24,10 @@
     amplitude = transmission.astype(jnp.float32)
     partial_value = jnp.sum(amplitude * amplitude * power, axis=0)
     partial_value = partial_value / jnp.float32(freq_total)
-    ambiguity = lax.psum(partial_value, "freq")
+    count_2, ambiguity = (lax.axis_size("freq"), partial_value)
+    for far in [1 << k for k in range(count_2.bit_length() - 1)]:
+        pairs = [(i, i ^ far) for i in range(count_2)]
+        ambiguity = ambiguity + lax.ppermute(ambiguity, "freq", pairs)
     peak = lax.pmax(jnp.max(ambiguity), "cell")
     relative = ambiguity / jnp.maximum(peak, jnp.float32(1.0))
     return (ambiguity, relative)

time: 198 us -> 191 us (0.965)
  blocking collectives: 25.7 us -> 9.54 us
  waiting for transfers between devices: 92.8 us -> 98.2 us
  starting transfers between devices: 0.04 us -> 4 us
    psum x1 -> x0, blocking collectives: 16.2 us -> none  [shards(): ambiguity = lax.psum(partial_value, 'freq')]
    ppermute x0 -> x3, waiting for transfers between devices: none -> 5.33 us  [shards(): ambiguity = ambiguity + lax.ppermute(ambiguity, 'freq', pairs)]
    ppermute x0 -> x3, starting transfers between devices: none -> 3.96 us  [shards(): ambiguity = ambiguity + lax.ppermute(ambiguity, 'freq', pairs)]
  transfers between devices with their start and end apart: 1 -> 4, of which waited for: 1 -> 4; matrix products, arithmetic and copies ran while one was open for 0% -> 0% of each run, Pallas kernels for 0% -> 0%
where the time goes in v1:
time: 191 us
  waiting for transfers between devices  98.2 us (51%)
  matrix products  35.5 us (19%)
  other arithmetic  28.8 us (15%)
  between operations  14.7 us (8%)
  blocking collectives  9.54 us (5%)
  starting transfers between devices  4 us (2%)
    all_gather x1, waiting for transfers between devices, shards(): lax.all_gather(covariance, 'cell', axis=2, tiled=True)  92.2 us
    reduce_sum x1, other arithmetic, quadratic(): jnp.sum(row_fields[:, 0] * image_re + row_fields[:, 1] * image_im, axis=1)  27.6 us
    dot_general x1, matrix products, quadratic(): jnp.einsum('fij,fjc->fic', stacked, col_fields[:, 1], preferred_element_t...  17.7 us
    dot_general x1, matrix products, quadratic(): jnp.einsum('fij,fjc->fic', stacked, col_fields[:, 0], preferred_element_t...  17.7 us
    pmax x1, blocking collectives, shards(): peak = lax.pmax(jnp.max(ambiguity), 'cell')  9.54 us
    ppermute x3, waiting for transfers between devices, shards(): ambiguity = ambiguity + lax.ppermute(ambiguity, 'freq', pairs)  5.33 us
    ppermute x3, starting transfers between devices, shards(): ambiguity = ambiguity + lax.ppermute(ambiguity, 'freq', pairs)  3.96 us
  transfers between devices with their start and end apart: 4, of which 4 were waited for; matrix products, arithmetic and copies ran while one was open for 0% of the time, Pallas kernels for 0%

profile of v1, /device:TPU:0, one launch (start us, length us, event | category | flops | bytes accessed | tf_op | source)
XLA Modules:
  0.0 190.7 jit_solution(9695983650593079534)
XLA Ops:
  7.2 0.0 all-gather.2.cloned.1.call-start
  7.2 0.7 all-gather.2.cloned.1.call-update
  7.9 92.2 %all-gather.2.cloned.1.call-done = bf16[32,2,256,256]{3,2,1,0:T(8,128)(2,1)} async-done(((bf16[32,2,64,256]{3,2,1,0:T(8,128)(2,1)}), bf16[32,2,256,256]{3,2,1,0:T(8,128)(2,1)}) %all-gather.2.cloned.1.call-update) | async-done | bytes 8388624 | tf_op jit(solution)/shard_map/all_gather | solution.py:23
  100.1 17.7 %fusion.4 = f32[32,512,512]{2,1,0:T(8,128)} fusion(bf16[32,512,256]{2,1,0:T(8,128)(2,1)} %bitcast.15, bf16[32,2,256,512]{3,2,1,0:T(8,128)(2,1)} %param.4), kind=kOutput, calls=%fused_computation.6 | convolution fusion | flops 4294967296 | bytes 50331648 | tf_op jit(solution)/shard_map/fij,fjc->fic/dot_general | solution.py:13
  117.8 17.7 %fusion.6 = f32[32,512,512]{2,1,0:T(8,128)} fusion(bf16[32,512,256]{2,1,0:T(8,128)(2,1)} %bitcast.16, bf16[32,2,256,512]{3,2,1,0:T(8,128)(2,1)} %param.4), kind=kOutput, calls=%fused_computation.8 | convolution fusion | flops 4294967296 | bytes 50331648 | tf_op jit(solution)/shard_map/fij,fjc->fic/dot_general | solution.py:10
  135.5 0.0 copy-start
  135.5 27.6 %fusion.2 = f32[32,512]{1,0:T(8,128)S(1)} fusion(f32[32,512,512]{2,1,0:T(8,128)} %fusion.4, f32[32,512,512]{2,1,0:T(8,128)} %fusion.6, bf16[32,2,256,512]{3,2,1,0:T(8,128)(2,1)} %param.4), kind=kLoop, calls=%fused_computation.3 | loop fusion | flops 33538048 | bytes 83951616 | tf_op jit(solution)/shard_map/reduce_sum | solution.py:18
  163.1 0.0 copy-done
  163.2 0.1 collective-permute-start
  163.3 1.1 collective-permute-done
  164.4 1.5 collective-permute-start.1
  165.9 2.1 %collective-permute-done.1 = f32[512]{0:T(512)S(1)} collective-permute-done((f32[512]{0:T(512)S(1)}, f32[512]{0:T(512)S(1)}, u32[]{:S(2)}, u32[]{:S(2)}) %collective-permute-start.1) | collective-permute-done | bytes 2080 | tf_op jit(solution)/shard_map/ppermute | solution.py:30
  168.0 2.4 %collective-permute-start.2 = (f32[512]{0:T(512)S(1)}, f32[512]{0:T(512)S(1)}, u32[]{:S(2)}, u32[]{:S(2)}) collective-permute-start(f32[512]{0:T(512)S(1)} %add.18), channel_id=1, source_target_pairs={{0,16},{4,20},{8,24},{12,28},{16,0},{20,4},{24,8},{28,12},{1,17},{... | collective-permute-start | bytes 6152 | tf_op jit(solution)/shard_map/ppermute | solution.py:30
  170.4 2.1 %collective-permute-done.2 = f32[512]{0:T(512)S(1)} collective-permute-done((f32[512]{0:T(512)S(1)}, f32[512]{0:T(512)S(1)}, u32[]{:S(2)}, u32[]{:S(2)}) %collective-permute-start.2) | collective-permute-done | bytes 2080 | tf_op jit(solution)/shard_map/ppermute | solution.py:30
  172.5 0.6 fusion.11
  173.1 0.0 copy-start.1
  173.1 9.5 %pmax.7 = f32[]{:T(128)} all-reduce(f32[]{:T(128)} %get-tuple-element.2), channel_id=1, replica_groups=mesh['freq'=8,'cell'=4] {'cell'}, use_global_device_ids=true, to_apply=%region_3.0 | all-reduce | flops 1 | bytes 8 | tf_op jit(solution)/shard_map/pmax | solution.py:31
  183.3 0.6 broadcast_divide_fusion
  183.9 0.0 copy-done.1
  (4 shorter events, 0.0 us)
Async XLA Ops:
  7.2 92.9 %all-gather.2.cloned.1.call-start = ((), (), s32[]{:S(2)}) async-start(), calls=%async_computation | async-start | bytes 10485760 | tf_op jit(solution)/shard_map/all_gather | solution.py:23
  135.5 27.6 %copy-start = (bf16[32,512]{1,0:T(8,128)(2,1)S(1)}, bf16[32,512]{1,0:T(8,128)(2,1)}, u32[]{:S(2)}) copy-start(bf16[32,512]{1,0:T(8,128)(2,1)} %param.5) | copy-start | bytes 98308
  163.2 1.2 collective-permute-start
  164.4 3.6 %collective-permute-start.1 = (f32[512]{0:T(512)S(1)}, f32[512]{0:T(512)S(1)}, u32[]{:S(2)}, u32[]{:S(2)}) collective-permute-start(f32[512]{0:T(512)S(1)} %fusion.10), channel_id=1, source_target_pairs={{0,8},{4,12},{8,0},{12,4},{16,24},{20,28},{24,16},{28,20},{1,9},{5... | collective-permute-start | bytes 6152 | tf_op jit(solution)/shard_map/ppermute | solution.py:30
  168.0 4.5 %collective-permute-start.2 = (f32[512]{0:T(512)S(1)}, f32[512]{0:T(512)S(1)}, u32[]{:S(2)}, u32[]{:S(2)}) collective-permute-start(f32[512]{0:T(512)S(1)} %add.18), channel_id=1, source_target_pairs={{0,16},{4,20},{8,24},{12,28},{16,0},{20,4},{24,8},{28,12},{1,17},{... | collective-permute-start | bytes 6152 | tf_op jit(solution)/shard_map/ppermute | solution.py:30
  173.1 10.8 %copy-start.1 = (f32[512]{0:T(512)}, f32[512]{0:T(512)S(1)}, u32[]{:S(2)}) copy-start(f32[512]{0:T(512)S(1)} %get-tuple-element.3) | copy-start | bytes 6148
Sparse Core Ops, SparseCore 0:
  9.8 90.1 all-gather.1
